TPU v7x, 32 devices: a whole 2x2x4 slice. The times are simulated.
32 devices in a mesh: section: 4 (over y, x), dp: 8 (over z, core).
Axes of the slice: x: 2, y: 2, z: 4, core: 2. Of those that a mesh axis runs over, the one named last changes fastest.
Arguments:
- descriptors: bfloat16 [4, 4096, 1024], P(None, 'dp'), may hold values from -6 to 6
- layer_weight: bfloat16 [4, 8, 1024, 1024], P('section', None, 'dp'), may hold values from -0.25 to 0.25
- layer_bias: float32 [4, 8, 1024], P('section'), may hold values from -3 to 3
- readout: float32 [8, 1024], replicated, may hold values from -0.75 to 0.75
- self_energy: float32 [8], replicated, may hold values from -2 to -0.5
- tile_species: int32 [4, 32], P(None, 'dp'), may hold values from 0 to 7
- tile_fill: int32 [4, 32], P(None, 'dp'), may hold values from 1 to 128
Outputs:
- atom_energy: float32 [4, 4096], P('section', 'dp')
- energy: float32 [4], replicated
All inputs are finite; a program needn't handle non-finite values.
Results may differ from a plain program's by a relative error of at most 0.0044.
Values may be sent and summed in bfloat16 or wider, within the bound.
No kernel may reach another device: no remote copies, remote signals or barrier semaphores. Data moves between devices by JAX's collectives and lax.ppermute only.
A program may use at most 128 MiB of HBM per device.

v0:
```python
import jax
import jax.numpy as jnp
from jax import lax
from jax.sharding import PartitionSpec as P


def shifted(block, axis, distance):
    devices = range(lax.axis_size(axis))
    route = [(i - distance, i) for i in devices if i - distance in devices]
    return lax.ppermute(block, axis, route)


def smooth_unit(value):
    return jnp.maximum(value, 0.0) + jnp.minimum(jnp.expm1(jnp.minimum(value, 0.0)), 0.0)


def grouped_product(source, weights, species):
    chosen = jnp.take(weights, species, axis=0)
    return jnp.einsum("tai,tio->tao", source, chosen, preferred_element_type=jnp.float32)


def table_rows(onehot, table):
    return jnp.dot(onehot, table, precision=lax.Precision.HIGHEST)


def shards(descriptors, layer_weight, layer_bias, readout, self_energy, tile_species, tile_fill):
    sections = lax.axis_size("section")
    position = lax.axis_index("section")
    batches, atoms_dev, width = descriptors.shape
    tiles_dev = tile_species.shape[1]
    tile = atoms_dev // tiles_dev
    kinds = readout.shape[0]
    atoms_all = atoms_dev * lax.axis_size("dp")
    total_steps = batches + sections - 1
    bias = layer_bias[0]
    is_last = position == sections - 1
    kind_ids = jnp.arange(kinds, dtype=jnp.int32)
    slot_ids = jnp.arange(tile, dtype=jnp.int32)
    incoming = jnp.zeros((atoms_dev, width), jnp.bfloat16)
    stored = jnp.zeros((batches, atoms_dev), jnp.float32)
    energies = jnp.zeros((batches,), jnp.float32)
    weights = None
    for step in range(total_steps):
        batch = step - position
        valid = jnp.logical_and(batch >= 0, batch < batches)
        keep = jnp.logical_and(valid, is_last)
        index = jnp.clip(batch, 0, batches - 1)
        species = lax.dynamic_index_in_dim(tile_species, index, 0, keepdims=False)
        fill = lax.dynamic_index_in_dim(tile_fill, index, 0, keepdims=False)
        first = descriptors[min(step, batches - 1)]
        source = jnp.where(position == 0, first, incoming).reshape(tiles_dev, tile, width)
        if step == 0:
            weights = lax.all_gather(layer_weight[0], "dp", axis=1, tiled=True)
            product = grouped_product(source, weights, species)
        else:
            product = grouped_product(source, weights, species)
        onehot = (species[:, None] == kind_ids[None, :]).astype(jnp.float32)
        active = smooth_unit(product + table_rows(onehot, bias)[:, None, :])
        readout_rows = table_rows(onehot, readout)
        offsets = table_rows(onehot, self_energy[:, None])
        values = jnp.sum(active * readout_rows[:, None, :], axis=-1) + offsets
        present = slot_ids[None, :] < fill[:, None]
        values = jnp.where(jnp.logical_and(present, keep), values, jnp.float32(0.0)).reshape(
            atoms_dev
        )
        stored = stored.at[index].add(values)
        term = jnp.sum(values) / atoms_all
        finished = step - (sections - 1)
        if 0 <= finished < batches:
            energies = energies.at[finished].set(lax.psum(term, ("section", "dp")))
        if step < total_steps - 1:
            incoming = shifted(active.astype(jnp.bfloat16).reshape(atoms_dev, width), "section", 1)
    received = lax.all_to_all(stored, "section", split_axis=0, concat_axis=0, tiled=True)
    mine = received[sections - 1]
    return (mine[None, :], energies)


def solution(mesh):
    placed = (
        P(None, "dp", None),
        P("section", None, "dp", None),
        P("section", None, None),
        P(),
        P(),
        P(None, "dp"),
        P(None, "dp"),
    )
    return jax.shard_map(
        shards, mesh=mesh, in_specs=placed, out_specs=(P("section", "dp"), P()), check_vma=False
    )
```

profile of v0, /device:TPU:12, one launch (start us, length us, event | category | flops | bytes accessed | tf_op | source)
XLA Modules:
  0.0 464.9 jit_solution(16702947367663745943)
XLA Ops:
  12.9 146.2 %all-gather.3.cloned.1.call-done = bf16[1,8,1024,1024]{3,2,1,0:T(8,128)(2,1)} async-done(((bf16[1,8,128,1024]{3,2,1,0:T(8,128)(2,1)}), bf16[1,8,1024,1024]{3,2,1,0:T(8,128)(2,1)}) %all-gather.3.cloned.1.call-update) | async-done | bytes 16777232 | tf_op jit(solution)/shard_map/all_gather | solution.py:53
  159.1 11.7 %fusion.131 = (bf16[8,512,1024]{2,1,0:T(8,128)(2,1)}, bf16[8,512,1024]{2,1,0:T(8,128)(2,1)}) fusion(bf16[8,1024,1024]{2,1,0:T(8,128)(2,1)} %bitcast.146), kind=kLoop, calls=%fused_computation.259 | loop fusion | bytes 33554432 | tf_op jit(solution)/shard_map/jit(_take)/gather | solution.py:18
  170.8 6.2 %gather_fusion = bf16[4,512,1024]{2,1,0:T(8,128)(2,1)} fusion(bf16[8,512,1024]{2,1,0:T(8,128)(2,1)} %get-tuple-element.168, s32[1024]{0:T(1024)S(1)} %pad_clamp_fusion.6), kind=kCustom, calls=%fused_computation.clone | custom fusion | bytes 8388624 | tf_op jit(solution)/shard_map/jit(_take)/gather | solution.py:18
  176.9 6.1 %gather_fusion.1 = bf16[4,512,1024]{2,1,0:T(8,128)(2,1)} fusion(bf16[8,512,1024]{2,1,0:T(8,128)(2,1)} %get-tuple-element.169, s32[1024]{0:T(1024)S(1)} %pad_clamp_fusion.6), kind=kCustom, calls=%fused_computation.1.clone | custom fusion | bytes 8388624 | tf_op jit(solution)/shard_map/jit(_take)/gather | solution.py:18
  193.5 6.2 %gather_fusion.2 = bf16[4,512,1024]{2,1,0:T(8,128)(2,1)} fusion(bf16[8,512,1024]{2,1,0:T(8,128)(2,1)} %get-tuple-element.168, s32[1024]{0:T(1024)S(1)} %pad_clamp_fusion.5), kind=kCustom, calls=%fused_computation.2.clone | custom fusion | bytes 8388624 | tf_op jit(solution)/shard_map/jit(_take)/gather | solution.py:18
  199.7 6.1 %gather_fusion.3 = bf16[4,512,1024]{2,1,0:T(8,128)(2,1)} fusion(bf16[8,512,1024]{2,1,0:T(8,128)(2,1)} %get-tuple-element.169, s32[1024]{0:T(1024)S(1)} %pad_clamp_fusion.5), kind=kCustom, calls=%fused_computation.3.clone | custom fusion | bytes 8388624 | tf_op jit(solution)/shard_map/jit(_take)/gather | solution.py:18
  205.8 10.8 %collective-permute-done = bf16[512,1024]{1,0:T(8,128)(2,1)S(1)} collective-permute-done((bf16[512,1024]{1,0:T(8,128)(2,1)S(1)}, bf16[512,1024]{1,0:T(8,128)(2,1)S(1)}, u32[]{:S(2)}, u32[]{:S(2)}) %collective-permute-start) | collective-permute-done | bytes 1048608 | tf_op jit(solution)/shard_map/ppermute | solution.py:10
  217.9 5.4 %fusion.136 = (bf16[4,128,1024]{2,1,0:T(8,128)(2,1)S(1)}, f32[4,128]{1,0:T(4,128)S(1)}) fusion(f32[4,1024]{1,0:T(4,128)S(1)} %fusion.55, f32[4,1024]{1,0:T(4,128)S(1)} %fusion.45, bf16[4,128,1024]{2,1,0:T(8,128)(2,1)S(1)} %bitcast.148, bf16[4,512,1024]{2,1,0:T(8,128)(2,1)} %gather_fusion.3, bf16[4,512,1024]{2,1,0:T(8,128)(2,1)} %gather_fusion.2, ...), kind=kOutput, calls=%fused_computation.264 | convolution fusion | flops 1098907136 | bytes 10520580 | tf_op jit(solution)/shard_map/tai,tio->tao/dot_general | solution.py:19
  227.0 6.2 %gather_fusion.4 = bf16[4,512,1024]{2,1,0:T(8,128)(2,1)} fusion(bf16[8,512,1024]{2,1,0:T(8,128)(2,1)} %get-tuple-element.168, s32[1024]{0:T(1024)S(1)} %pad_clamp_fusion.4), kind=kCustom, calls=%fused_computation.4.clone | custom fusion | bytes 8388624 | tf_op jit(solution)/shard_map/jit(_take)/gather | solution.py:18
  233.2 6.1 %gather_fusion.5 = bf16[4,512,1024]{2,1,0:T(8,128)(2,1)} fusion(bf16[8,512,1024]{2,1,0:T(8,128)(2,1)} %get-tuple-element.169, s32[1024]{0:T(1024)S(1)} %pad_clamp_fusion.4), kind=kCustom, calls=%fused_computation.5.clone | custom fusion | bytes 8388624 | tf_op jit(solution)/shard_map/jit(_take)/gather | solution.py:18
  239.4 11.2 %collective-permute-done.1 = bf16[512,1024]{1,0:T(8,128)(2,1)S(1)} collective-permute-done((bf16[512,1024]{1,0:T(8,128)(2,1)S(1)}, bf16[512,1024]{1,0:T(8,128)(2,1)S(1)}, u32[]{:S(2)}, u32[]{:S(2)}) %collective-permute-start.1) | collective-permute-done | bytes 1048608 | tf_op jit(solution)/shard_map/ppermute | solution.py:10
  260.3 6.2 %gather_fusion.6 = bf16[4,512,1024]{2,1,0:T(8,128)(2,1)} fusion(bf16[8,512,1024]{2,1,0:T(8,128)(2,1)} %get-tuple-element.168, s32[1024]{0:T(1024)S(1)} %pad_clamp_fusion.3), kind=kCustom, calls=%fused_computation.6.clone | custom fusion | bytes 8388624 | tf_op jit(solution)/shard_map/jit(_take)/gather | solution.py:18
  266.5 6.1 %gather_fusion.7 = bf16[4,512,1024]{2,1,0:T(8,128)(2,1)} fusion(bf16[8,512,1024]{2,1,0:T(8,128)(2,1)} %get-tuple-element.169, s32[1024]{0:T(1024)S(1)} %pad_clamp_fusion.3), kind=kCustom, calls=%fused_computation.7.clone | custom fusion | bytes 8388624 | tf_op jit(solution)/shard_map/jit(_take)/gather | solution.py:18
  272.6 11.2 %collective-permute-done.2 = bf16[512,1024]{1,0:T(8,128)(2,1)S(1)} collective-permute-done((bf16[512,1024]{1,0:T(8,128)(2,1)S(1)}, bf16[512,1024]{1,0:T(8,128)(2,1)S(1)}, u32[]{:S(2)}, u32[]{:S(2)}) %collective-permute-start.2) | collective-permute-done | bytes 1048608 | tf_op jit(solution)/shard_map/ppermute | solution.py:10
  285.1 5.4 %fusion.134 = (bf16[4,128,1024]{2,1,0:T(8,128)(2,1)S(1)}, f32[4,128]{1,0:T(4,128)S(1)}) fusion(f32[4,1024]{1,0:T(4,128)S(1)} %fusion.53, f32[4,1024]{1,0:T(4,128)S(1)} %fusion.41, bf16[4,128,1024]{2,1,0:T(8,128)(2,1)S(1)} %bitcast.150, bf16[4,512,1024]{2,1,0:T(8,128)(2,1)} %gather_fusion.7, bf16[4,512,1024]{2,1,0:T(8,128)(2,1)} %gather_fusion.6, ...), kind=kOutput, calls=%fused_computation.262 | convolution fusion | flops 1098907136 | bytes 10520580 | tf_op jit(solution)/shard_map/tai,tio->tao/dot_general | solution.py:19
  293.5 6.3 %gather_fusion.8 = bf16[4,512,1024]{2,1,0:T(8,128)(2,1)} fusion(bf16[8,512,1024]{2,1,0:T(8,128)(2,1)} %get-tuple-element.168, s32[1024]{0:T(1024)S(1)} %pad_clamp_fusion.2), kind=kCustom, calls=%fused_computation.8.clone | custom fusion | bytes 8388624 | tf_op jit(solution)/shard_map/jit(_take)/gather | solution.py:18
  299.8 6.1 %gather_fusion.9 = bf16[4,512,1024]{2,1,0:T(8,128)(2,1)} fusion(bf16[8,512,1024]{2,1,0:T(8,128)(2,1)} %get-tuple-element.169, s32[1024]{0:T(1024)S(1)} %pad_clamp_fusion.2), kind=kCustom, calls=%fused_computation.9.clone | custom fusion | bytes 8388624 | tf_op jit(solution)/shard_map/jit(_take)/gather | solution.py:18
  305.9 6.2 %gather_fusion.10 = bf16[4,512,1024]{2,1,0:T(8,128)(2,1)} fusion(bf16[8,512,1024]{2,1,0:T(8,128)(2,1)} %get-tuple-element.168, s32[1024]{0:T(1024)S(1)} %pad_clamp_fusion.1), kind=kCustom, calls=%fused_computation.10.clone | custom fusion | bytes 8388624 | tf_op jit(solution)/shard_map/jit(_take)/gather | solution.py:18
  312.1 6.2 %gather_fusion.11 = bf16[4,512,1024]{2,1,0:T(8,128)(2,1)} fusion(bf16[8,512,1024]{2,1,0:T(8,128)(2,1)} %get-tuple-element.169, s32[1024]{0:T(1024)S(1)} %pad_clamp_fusion.1), kind=kCustom, calls=%fused_computation.11.clone | custom fusion | bytes 8388624 | tf_op jit(solution)/shard_map/jit(_take)/gather | solution.py:18
  318.2 6.1 %gather_fusion.12 = bf16[4,512,1024]{2,1,0:T(8,128)(2,1)} fusion(bf16[8,512,1024]{2,1,0:T(8,128)(2,1)} %get-tuple-element.168, s32[1024]{0:T(1024)S(1)} %pad_clamp_fusion), kind=kCustom, calls=%fused_computation.12.clone | custom fusion | bytes 8388624 | tf_op jit(solution)/shard_map/jit(_take)/gather | solution.py:18
  324.4 6.2 %gather_fusion.13 = bf16[4,512,1024]{2,1,0:T(8,128)(2,1)} fusion(bf16[8,512,1024]{2,1,0:T(8,128)(2,1)} %get-tuple-element.169, s32[1024]{0:T(1024)S(1)} %pad_clamp_fusion), kind=kCustom, calls=%fused_computation.13.clone | custom fusion | bytes 8388624 | tf_op jit(solution)/shard_map/jit(_take)/gather | solution.py:18
  342.2 21.4 %collective-permute-done.4 = bf16[512,1024]{1,0:T(8,128)(2,1)S(1)} collective-permute-done((bf16[512,1024]{1,0:T(8,128)(2,1)S(1)}, bf16[512,1024]{1,0:T(8,128)(2,1)S(1)}, u32[]{:S(2)}, u32[]{:S(2)}) %collective-permute-start.4) | collective-permute-done | bytes 1048608 | tf_op jit(solution)/shard_map/ppermute | solution.py:10
  376.3 18.7 %collective-permute-done.5 = bf16[512,1024]{1,0:T(8,128)(2,1)S(1)} collective-permute-done((bf16[512,1024]{1,0:T(8,128)(2,1)S(1)}, bf16[512,1024]{1,0:T(8,128)(2,1)S(1)}, u32[]{:S(2)}, u32[]{:S(2)}) %collective-permute-start.5) | collective-permute-done | bytes 1048608 | tf_op jit(solution)/shard_map/ppermute | solution.py:10
  409.5 45.5 %all-reduce.1 = (f32[1]{0:T(128)}, f32[1]{0:T(128)}, f32[1]{0:T(128)}, f32[1]{0:T(128)}) all-reduce(f32[1]{0:T(128)} %bitcast.62, f32[1]{0:T(128)} %bitcast.63, f32[1]{0:T(128)} %bitcast.64, f32[1]{0:T(128)} %bitcast.65), channel_id=1, replica_groups=mesh['section'=4,'dp'=8] {'section','dp'}, use_global_device_ids=true, to_apply=%region_15.17 | all-reduce | flops 4 | bytes 32 | tf_op jit(solution)/shard_map/psum | solution.py:70
  (97 shorter events, 74.2 us)
Async XLA Ops:
  7.2 3.3 copy-start
  7.2 151.9 %all-gather.3.cloned.1.call-start = ((), (), s32[]{:S(2)}) async-start(), calls=%async_computation.1 | async-start | bytes 18874368 | tf_op jit(solution)/shard_map/all_gather | solution.py:53
  183.1 8.8 %copy-start.2 = (s32[2]{0:T(128)S(1)}, s32[2]{0:T(128)}, u32[]{:S(2)}) copy-start(s32[2]{0:T(128)} %constant.301.clone.1) | copy-start | bytes 28
  183.1 9.6 %copy-start.4 = (f32[8]{0:T(128)S(1)}, f32[8]{0:T(128)}, u32[]{:S(2)}) copy-start(f32[8]{0:T(128)} %param.35) | copy-start | bytes 100
  183.1 10.2 %copy-start.3 = (f32[8,1024]{1,0:T(8,128)S(1)}, f32[8,1024]{1,0:T(8,128)}, u32[]{:S(2)}) copy-start(f32[8,1024]{1,0:T(8,128)} %param.34) | copy-start | bytes 98308
  188.5 28.1 %collective-permute-start = (bf16[512,1024]{1,0:T(8,128)(2,1)S(1)}, bf16[512,1024]{1,0:T(8,128)(2,1)S(1)}, u32[]{:S(2)}, u32[]{:S(2)}) collective-permute-start(bf16[512,1024]{1,0:T(8,128)(2,1)S(1)} %bitcast.164), channel_id=1, source_target_pairs={{0,8},{8,16},{16,24},{1,9},{9,17},{17,25},{2,10},{10,18},{18,26},{... | collective-permute-start | bytes 3145736 | tf_op jit(solution)/shard_map/ppermute | solution.py:10
  223.3 27.3 %collective-permute-start.1 = (bf16[512,1024]{1,0:T(8,128)(2,1)S(1)}, bf16[512,1024]{1,0:T(8,128)(2,1)S(1)}, u32[]{:S(2)}, u32[]{:S(2)}) collective-permute-start(bf16[512,1024]{1,0:T(8,128)(2,1)S(1)} %bitcast.166), channel_id=1, source_target_pairs={{0,8},{8,16},{16,24},{1,9},{9,17},{17,25},{2,10},{10,18},{18,26},{... | collective-permute-start | bytes 3145736 | tf_op jit(solution)/shard_map/ppermute | solution.py:10
  257.4 26.4 %collective-permute-start.2 = (bf16[512,1024]{1,0:T(8,128)(2,1)S(1)}, bf16[512,1024]{1,0:T(8,128)(2,1)S(1)}, u32[]{:S(2)}, u32[]{:S(2)}) collective-permute-start(bf16[512,1024]{1,0:T(8,128)(2,1)S(1)} %bitcast.165), channel_id=1, source_target_pairs={{0,8},{8,16},{16,24},{1,9},{9,17},{17,25},{2,10},{10,18},{18,26},{... | collective-permute-start | bytes 3145736 | tf_op jit(solution)/shard_map/ppermute | solution.py:10
  285.1 7.5 %copy-start.1 = (s32[4,4]{1,0:T(4,128)S(1)}, s32[4,4]{1,0:T(4,128)}, u32[]{:S(2)}) copy-start(s32[4,4]{1,0:T(4,128)} %param.37) | copy-start | bytes 196
  290.5 40.7 %collective-permute-start.3 = (bf16[512,1024]{1,0:T(8,128)(2,1)S(1)}, bf16[512,1024]{1,0:T(8,128)(2,1)S(1)}, u32[]{:S(2)}, u32[]{:S(2)}) collective-permute-start(bf16[512,1024]{1,0:T(8,128)(2,1)S(1)} %bitcast.161), channel_id=1, source_target_pairs={{0,8},{8,16},{16,24},{1,9},{9,17},{17,25},{2,10},{10,18},{18,26},{... | collective-permute-start | bytes 3145736 | tf_op jit(solution)/shard_map/ppermute | solution.py:10
  338.0 25.6 %collective-permute-start.4 = (bf16[512,1024]{1,0:T(8,128)(2,1)S(1)}, bf16[512,1024]{1,0:T(8,128)(2,1)S(1)}, u32[]{:S(2)}, u32[]{:S(2)}) collective-permute-start(bf16[512,1024]{1,0:T(8,128)(2,1)S(1)} %bitcast.163), channel_id=1, source_target_pairs={{0,8},{8,16},{16,24},{1,9},{9,17},{17,25},{2,10},{10,18},{18,26},{... | collective-permute-start | bytes 3145736 | tf_op jit(solution)/shard_map/ppermute | solution.py:10
  370.4 24.7 %collective-permute-start.5 = (bf16[512,1024]{1,0:T(8,128)(2,1)S(1)}, bf16[512,1024]{1,0:T(8,128)(2,1)S(1)}, u32[]{:S(2)}, u32[]{:S(2)}) collective-permute-start(bf16[512,1024]{1,0:T(8,128)(2,1)S(1)} %bitcast.162), channel_id=1, source_target_pairs={{0,8},{8,16},{16,24},{1,9},{9,17},{17,25},{2,10},{10,18},{18,26},{... | collective-permute-start | bytes 3145736 | tf_op jit(solution)/shard_map/ppermute | solution.py:10
  403.7 53.8 %all-to-all-start = ((f32[4,1,512]{2,1,0:T(1,128)}), f32[4,1,512]{2,1,0:T(1,128)S(1)}, u32[]{:S(2)}, u32[]{:S(2)}) async-start(f32[4,1,512]{2,1,0:T(1,128)} %constant_dynamic-update-slice_fusion), calls=%async_computation | async-start | bytes 16384 | tf_op jit(solution)/shard_map/all_to_all | solution.py:73
  457.4 0.6 copy-start.5
Sparse Core Ops, SparseCore 0:
  9.6 149.4 all-gather.2
where the time goes:
time: 466 us; the launch traced here: 465 us
  waiting for transfers between devices  220 us (47%)
  local copies, waits for them, and re-layouts  102 us (22%)
  blocking collectives  45.5 us (10%)
  matrix products  42.8 us (9%)
  other arithmetic  20.5 us (4%)
  starting transfers between devices  17.1 us (4%)
  between operations  17 us (4%)
    all_gather x1, waiting for transfers between devices, shards(): weights = lax.all_gather(layer_weight[0], 'dp', axis=1, tiled=True)  146 us
    gather x15, local copies, waits for them, and re-layouts, grouped_product(): chosen = jnp.take(weights, species, axis=0)  97.9 us
    ppermute x6, waiting for transfers between devices, shifted(): return lax.ppermute(block, axis, route)  73.3 us
    psum x1, blocking collectives, shards(): energies = energies.at[finished].set(lax.psum(term, ('section', 'dp')))  45.5 us
    dot_general x7, matrix products, grouped_product(): jnp.einsum('tai,tio->tao', source, chosen, preferred_element_type=jnp.flo...  37.9 us
    ppermute x6, starting transfers between devices, shifted(): return lax.ppermute(block, axis, route)  13.7 us
  transfers between devices with their start and end apart: 8, of which 6 were waited for; matrix products, arithmetic and copies ran while one was open for 20% of the time, Pallas kernels for 0%

commit v1 on v0

--- a/solution.py
+++ b/solution.py
@@ -67,7 +67,7 @@
         term = jnp.sum(values) / atoms_all
         finished = step - (sections - 1)
         if 0 <= finished < batches:
-            energies = energies.at[finished].set(lax.psum(term, ("section", "dp")))
+            energies = energies.at[finished].set(lax.psum(lax.psum(term, "dp"), "section"))
         if step < total_steps - 1:
             incoming = shifted(active.astype(jnp.bfloat16).reshape(atoms_dev, width), "section", 1)
     received = lax.all_to_all(stored, "section", split_axis=0, concat_axis=0, tiled=True)

time: 466 us -> 450 us (0.966); the launches traced: 465 us -> 443 us
  blocking collectives: 45.5 us -> 23 us
    psum x1 -> x2, blocking collectives: 45.5 us -> 23 us  [the longest x1 13.4 us: shards(): lax.psum(term, 'dp')]
  transfers between devices with their start and end apart: 8 -> 8, of which waited for: 6 -> 6; matrix products, arithmetic and copies ran while one was open for 20% -> 21% of each run, Pallas kernels for 0% -> 0%
where the time goes in v1:
time: 450 us; the launch traced here: 443 us
  waiting for transfers between devices  220 us (49%)
  local copies, waits for them, and re-layouts  102 us (23%)
  matrix products  42.8 us (10%)
  blocking collectives  23 us (5%)
  other arithmetic  20.5 us (5%)
  starting transfers between devices  17.1 us (4%)
  between operations  17 us (4%)
    all_gather x1, waiting for transfers between devices, shards(): weights = lax.all_gather(layer_weight[0], 'dp', axis=1, tiled=True)  146 us
    gather x15, local copies, waits for them, and re-layouts, grouped_product(): chosen = jnp.take(weights, species, axis=0)  97.9 us
    ppermute x6, waiting for transfers between devices, shifted(): return lax.ppermute(block, axis, route)  73.3 us
    dot_general x7, matrix products, grouped_product(): jnp.einsum('tai,tio->tao', source, chosen, preferred_element_type=jnp.flo...  37.9 us
    ppermute x6, starting transfers between devices, shifted(): return lax.ppermute(block, axis, route)  13.7 us
    psum x1, blocking collectives, shards(): lax.psum(term, 'dp')  13.4 us
    psum x1, blocking collectives, shards(): lax.psum(lax.psum(term, 'dp'), 'section')  9.6 us
    select_n x7, other arithmetic, shards(): jnp.where(position == 0, first, incoming).reshape(tiles_dev, tile, width)  9.32 us
  transfers between devices with their start and end apart: 8, of which 6 were waited for; matrix products, arithmetic and copies ran while one was open for 21% of the time, Pallas kernels for 0%

profile of v1, /device:TPU:12, one launch (start us, length us, event | category | flops | bytes accessed | tf_op | source)
XLA Modules:
  0.0 442.5 jit_solution(5248178526483746721)
XLA Ops:
  12.9 146.2 %all-gather.3.cloned.1.call-done = bf16[1,8,1024,1024]{3,2,1,0:T(8,128)(2,1)} async-done(((bf16[1,8,128,1024]{3,2,1,0:T(8,128)(2,1)}), bf16[1,8,1024,1024]{3,2,1,0:T(8,128)(2,1)}) %all-gather.3.cloned.1.call-update) | async-done | bytes 16777232 | tf_op jit(solution)/shard_map/all_gather | solution.py:53
  159.1 11.7 %fusion.131 = (bf16[8,512,1024]{2,1,0:T(8,128)(2,1)}, bf16[8,512,1024]{2,1,0:T(8,128)(2,1)}) fusion(bf16[8,1024,1024]{2,1,0:T(8,128)(2,1)} %bitcast.146), kind=kLoop, calls=%fused_computation.259 | loop fusion | bytes 33554432 | tf_op jit(solution)/shard_map/jit(_take)/gather | solution.py:18
  170.8 6.2 %gather_fusion = bf16[4,512,1024]{2,1,0:T(8,128)(2,1)} fusion(bf16[8,512,1024]{2,1,0:T(8,128)(2,1)} %get-tuple-element.172, s32[1024]{0:T(1024)S(1)} %pad_clamp_fusion.6), kind=kCustom, calls=%fused_computation.clone | custom fusion | bytes 8388624 | tf_op jit(solution)/shard_map/jit(_take)/gather | solution.py:18
  176.9 6.1 %gather_fusion.1 = bf16[4,512,1024]{2,1,0:T(8,128)(2,1)} fusion(bf16[8,512,1024]{2,1,0:T(8,128)(2,1)} %get-tuple-element.173, s32[1024]{0:T(1024)S(1)} %pad_clamp_fusion.6), kind=kCustom, calls=%fused_computation.1.clone | custom fusion | bytes 8388624 | tf_op jit(solution)/shard_map/jit(_take)/gather | solution.py:18
  193.5 6.2 %gather_fusion.2 = bf16[4,512,1024]{2,1,0:T(8,128)(2,1)} fusion(bf16[8,512,1024]{2,1,0:T(8,128)(2,1)} %get-tuple-element.172, s32[1024]{0:T(1024)S(1)} %pad_clamp_fusion.5), kind=kCustom, calls=%fused_computation.2.clone | custom fusion | bytes 8388624 | tf_op jit(solution)/shard_map/jit(_take)/gather | solution.py:18
  199.7 6.1 %gather_fusion.3 = bf16[4,512,1024]{2,1,0:T(8,128)(2,1)} fusion(bf16[8,512,1024]{2,1,0:T(8,128)(2,1)} %get-tuple-element.173, s32[1024]{0:T(1024)S(1)} %pad_clamp_fusion.5), kind=kCustom, calls=%fused_computation.3.clone | custom fusion | bytes 8388624 | tf_op jit(solution)/shard_map/jit(_take)/gather | solution.py:18
  205.8 10.8 %collective-permute-done = bf16[512,1024]{1,0:T(8,128)(2,1)S(1)} collective-permute-done((bf16[512,1024]{1,0:T(8,128)(2,1)S(1)}, bf16[512,1024]{1,0:T(8,128)(2,1)S(1)}, u32[]{:S(2)}, u32[]{:S(2)}) %collective-permute-start) | collective-permute-done | bytes 1048608 | tf_op jit(solution)/shard_map/ppermute | solution.py:10
  217.9 5.4 %fusion.136 = (bf16[4,128,1024]{2,1,0:T(8,128)(2,1)S(1)}, f32[4,128]{1,0:T(4,128)S(1)}) fusion(f32[4,1024]{1,0:T(4,128)S(1)} %fusion.55, f32[4,1024]{1,0:T(4,128)S(1)} %fusion.45, bf16[4,128,1024]{2,1,0:T(8,128)(2,1)S(1)} %bitcast.148, bf16[4,512,1024]{2,1,0:T(8,128)(2,1)} %gather_fusion.3, bf16[4,512,1024]{2,1,0:T(8,128)(2,1)} %gather_fusion.2, ...), kind=kOutput, calls=%fused_computation.264 | convolution fusion | flops 1098907136 | bytes 10520580 | tf_op jit(solution)/shard_map/tai,tio->tao/dot_general | solution.py:19
  227.0 6.2 %gather_fusion.4 = bf16[4,512,1024]{2,1,0:T(8,128)(2,1)} fusion(bf16[8,512,1024]{2,1,0:T(8,128)(2,1)} %get-tuple-element.172, s32[1024]{0:T(1024)S(1)} %pad_clamp_fusion.4), kind=kCustom, calls=%fused_computation.4.clone | custom fusion | bytes 8388624 | tf_op jit(solution)/shard_map/jit(_take)/gather | solution.py:18
  233.2 6.1 %gather_fusion.5 = bf16[4,512,1024]{2,1,0:T(8,128)(2,1)} fusion(bf16[8,512,1024]{2,1,0:T(8,128)(2,1)} %get-tuple-element.173, s32[1024]{0:T(1024)S(1)} %pad_clamp_fusion.4), kind=kCustom, calls=%fused_computation.5.clone | custom fusion | bytes 8388624 | tf_op jit(solution)/shard_map/jit(_take)/gather | solution.py:18
  239.4 11.2 %collective-permute-done.1 = bf16[512,1024]{1,0:T(8,128)(2,1)S(1)} collective-permute-done((bf16[512,1024]{1,0:T(8,128)(2,1)S(1)}, bf16[512,1024]{1,0:T(8,128)(2,1)S(1)}, u32[]{:S(2)}, u32[]{:S(2)}) %collective-permute-start.1) | collective-permute-done | bytes 1048608 | tf_op jit(solution)/shard_map/ppermute | solution.py:10
  260.3 6.2 %gather_fusion.6 = bf16[4,512,1024]{2,1,0:T(8,128)(2,1)} fusion(bf16[8,512,1024]{2,1,0:T(8,128)(2,1)} %get-tuple-element.172, s32[1024]{0:T(1024)S(1)} %pad_clamp_fusion.3), kind=kCustom, calls=%fused_computation.6.clone | custom fusion | bytes 8388624 | tf_op jit(solution)/shard_map/jit(_take)/gather | solution.py:18
  266.5 6.1 %gather_fusion.7 = bf16[4,512,1024]{2,1,0:T(8,128)(2,1)} fusion(bf16[8,512,1024]{2,1,0:T(8,128)(2,1)} %get-tuple-element.173, s32[1024]{0:T(1024)S(1)} %pad_clamp_fusion.3), kind=kCustom, calls=%fused_computation.7.clone | custom fusion | bytes 8388624 | tf_op jit(solution)/shard_map/jit(_take)/gather | solution.py:18
  272.6 11.2 %collective-permute-done.2 = bf16[512,1024]{1,0:T(8,128)(2,1)S(1)} collective-permute-done((bf16[512,1024]{1,0:T(8,128)(2,1)S(1)}, bf16[512,1024]{1,0:T(8,128)(2,1)S(1)}, u32[]{:S(2)}, u32[]{:S(2)}) %collective-permute-start.2) | collective-permute-done | bytes 1048608 | tf_op jit(solution)/shard_map/ppermute | solution.py:10
  293.5 6.3 %gather_fusion.8 = bf16[4,512,1024]{2,1,0:T(8,128)(2,1)} fusion(bf16[8,512,1024]{2,1,0:T(8,128)(2,1)} %get-tuple-element.172, s32[1024]{0:T(1024)S(1)} %pad_clamp_fusion.2), kind=kCustom, calls=%fused_computation.8.clone | custom fusion | bytes 8388624 | tf_op jit(solution)/shard_map/jit(_take)/gather | solution.py:18
  299.8 6.1 %gather_fusion.9 = bf16[4,512,1024]{2,1,0:T(8,128)(2,1)} fusion(bf16[8,512,1024]{2,1,0:T(8,128)(2,1)} %get-tuple-element.173, s32[1024]{0:T(1024)S(1)} %pad_clamp_fusion.2), kind=kCustom, calls=%fused_computation.9.clone | custom fusion | bytes 8388624 | tf_op jit(solution)/shard_map/jit(_take)/gather | solution.py:18
  305.9 6.2 %gather_fusion.10 = bf16[4,512,1024]{2,1,0:T(8,128)(2,1)} fusion(bf16[8,512,1024]{2,1,0:T(8,128)(2,1)} %get-tuple-element.172, s32[1024]{0:T(1024)S(1)} %pad_clamp_fusion.1), kind=kCustom, calls=%fused_computation.10.clone | custom fusion | bytes 8388624 | tf_op jit(solution)/shard_map/jit(_take)/gather | solution.py:18
  312.1 6.2 %gather_fusion.11 = bf16[4,512,1024]{2,1,0:T(8,128)(2,1)} fusion(bf16[8,512,1024]{2,1,0:T(8,128)(2,1)} %get-tuple-element.173, s32[1024]{0:T(1024)S(1)} %pad_clamp_fusion.1), kind=kCustom, calls=%fused_computation.11.clone | custom fusion | bytes 8388624 | tf_op jit(solution)/shard_map/jit(_take)/gather | solution.py:18
  318.2 6.1 %gather_fusion.12 = bf16[4,512,1024]{2,1,0:T(8,128)(2,1)} fusion(bf16[8,512,1024]{2,1,0:T(8,128)(2,1)} %get-tuple-element.172, s32[1024]{0:T(1024)S(1)} %pad_clamp_fusion), kind=kCustom, calls=%fused_computation.12.clone | custom fusion | bytes 8388624 | tf_op jit(solution)/shard_map/jit(_take)/gather | solution.py:18
  324.4 6.2 %gather_fusion.13 = bf16[4,512,1024]{2,1,0:T(8,128)(2,1)} fusion(bf16[8,512,1024]{2,1,0:T(8,128)(2,1)} %get-tuple-element.173, s32[1024]{0:T(1024)S(1)} %pad_clamp_fusion), kind=kCustom, calls=%fused_computation.13.clone | custom fusion | bytes 8388624 | tf_op jit(solution)/shard_map/jit(_take)/gather | solution.py:18
  342.2 21.4 %collective-permute-done.4 = bf16[512,1024]{1,0:T(8,128)(2,1)S(1)} collective-permute-done((bf16[512,1024]{1,0:T(8,128)(2,1)S(1)}, bf16[512,1024]{1,0:T(8,128)(2,1)S(1)}, u32[]{:S(2)}, u32[]{:S(2)}) %collective-permute-start.4) | collective-permute-done | bytes 1048608 | tf_op jit(solution)/shard_map/ppermute | solution.py:10
  376.3 18.7 %collective-permute-done.5 = bf16[512,1024]{1,0:T(8,128)(2,1)S(1)} collective-permute-done((bf16[512,1024]{1,0:T(8,128)(2,1)S(1)}, bf16[512,1024]{1,0:T(8,128)(2,1)S(1)}, u32[]{:S(2)}, u32[]{:S(2)}) %collective-permute-start.5) | collective-permute-done | bytes 1048608 | tf_op jit(solution)/shard_map/ppermute | solution.py:10
  409.5 13.4 %all-reduce.1 = (f32[]{:T(128)}, f32[]{:T(128)}, f32[]{:T(128)}, f32[]{:T(128)}) all-reduce(f32[]{:T(128)S(6)} %div.12, f32[]{:T(128)S(6)} %div.13, f32[]{:T(128)S(6)} %div.14, f32[]{:T(128)S(6)} %div.15), channel_id=1, replica_groups=mesh['section'=4,'dp'=8] {'dp'}, use_global_device_ids=true, to_apply=%region_15.17 | all-reduce | flops 4 | bytes 32 | tf_op jit(solution)/shard_map/psum | solution.py:70
  422.9 9.6 %all-reduce.2 = (f32[1]{0:T(128)}, f32[1]{0:T(128)}, f32[1]{0:T(128)}, f32[1]{0:T(128)}) all-reduce(f32[1]{0:T(128)} %bitcast.62, f32[1]{0:T(128)} %bitcast.63, f32[1]{0:T(128)} %bitcast.64, f32[1]{0:T(128)} %bitcast.65), channel_id=1, replica_groups=mesh['section'=4,'dp'=8] {'section'}, use_global_device_ids=true, to_apply=%region_16.18 | all-reduce | flops 4 | bytes 32 | tf_op jit(solution)/shard_map/psum | solution.py:70
  (98 shorter events, 79.7 us)
Async XLA Ops:
  7.2 3.3 copy-start
  7.2 151.9 %all-gather.3.cloned.1.call-start = ((), (), s32[]{:S(2)}) async-start(), calls=%async_computation.1 | async-start | bytes 18874368 | tf_op jit(solution)/shard_map/all_gather | solution.py:53
  183.1 8.8 %copy-start.2 = (s32[2]{0:T(128)S(1)}, s32[2]{0:T(128)}, u32[]{:S(2)}) copy-start(s32[2]{0:T(128)} %constant.301.clone.1) | copy-start | bytes 28
  183.1 9.6 %copy-start.4 = (f32[8]{0:T(128)S(1)}, f32[8]{0:T(128)}, u32[]{:S(2)}) copy-start(f32[8]{0:T(128)} %param.35) | copy-start | bytes 100
  183.1 10.2 %copy-start.3 = (f32[8,1024]{1,0:T(8,128)S(1)}, f32[8,1024]{1,0:T(8,128)}, u32[]{:S(2)}) copy-start(f32[8,1024]{1,0:T(8,128)} %param.34) | copy-start | bytes 98308
  188.5 28.1 %collective-permute-start = (bf16[512,1024]{1,0:T(8,128)(2,1)S(1)}, bf16[512,1024]{1,0:T(8,128)(2,1)S(1)}, u32[]{:S(2)}, u32[]{:S(2)}) collective-permute-start(bf16[512,1024]{1,0:T(8,128)(2,1)S(1)} %bitcast.164), channel_id=1, source_target_pairs={{0,8},{8,16},{16,24},{1,9},{9,17},{17,25},{2,10},{10,18},{18,26},{... | collective-permute-start | bytes 3145736 | tf_op jit(solution)/shard_map/ppermute | solution.py:10
  223.3 27.3 %collective-permute-start.1 = (bf16[512,1024]{1,0:T(8,128)(2,1)S(1)}, bf16[512,1024]{1,0:T(8,128)(2,1)S(1)}, u32[]{:S(2)}, u32[]{:S(2)}) collective-permute-start(bf16[512,1024]{1,0:T(8,128)(2,1)S(1)} %bitcast.166), channel_id=1, source_target_pairs={{0,8},{8,16},{16,24},{1,9},{9,17},{17,25},{2,10},{10,18},{18,26},{... | collective-permute-start | bytes 3145736 | tf_op jit(solution)/shard_map/ppermute | solution.py:10
  257.4 26.4 %collective-permute-start.2 = (bf16[512,1024]{1,0:T(8,128)(2,1)S(1)}, bf16[512,1024]{1,0:T(8,128)(2,1)S(1)}, u32[]{:S(2)}, u32[]{:S(2)}) collective-permute-start(bf16[512,1024]{1,0:T(8,128)(2,1)S(1)} %bitcast.165), channel_id=1, source_target_pairs={{0,8},{8,16},{16,24},{1,9},{9,17},{17,25},{2,10},{10,18},{18,26},{... | collective-permute-start | bytes 3145736 | tf_op jit(solution)/shard_map/ppermute | solution.py:10
  285.1 7.5 %copy-start.1 = (s32[4,4]{1,0:T(4,128)S(1)}, s32[4,4]{1,0:T(4,128)}, u32[]{:S(2)}) copy-start(s32[4,4]{1,0:T(4,128)} %param.37) | copy-start | bytes 196
  290.5 40.7 %collective-permute-start.3 = (bf16[512,1024]{1,0:T(8,128)(2,1)S(1)}, bf16[512,1024]{1,0:T(8,128)(2,1)S(1)}, u32[]{:S(2)}, u32[]{:S(2)}) collective-permute-start(bf16[512,1024]{1,0:T(8,128)(2,1)S(1)} %bitcast.161), channel_id=1, source_target_pairs={{0,8},{8,16},{16,24},{1,9},{9,17},{17,25},{2,10},{10,18},{18,26},{... | collective-permute-start | bytes 3145736 | tf_op jit(solution)/shard_map/ppermute | solution.py:10
  338.0 25.6 %collective-permute-start.4 = (bf16[512,1024]{1,0:T(8,128)(2,1)S(1)}, bf16[512,1024]{1,0:T(8,128)(2,1)S(1)}, u32[]{:S(2)}, u32[]{:S(2)}) collective-permute-start(bf16[512,1024]{1,0:T(8,128)(2,1)S(1)} %bitcast.163), channel_id=1, source_target_pairs={{0,8},{8,16},{16,24},{1,9},{9,17},{17,25},{2,10},{10,18},{18,26},{... | collective-permute-start | bytes 3145736 | tf_op jit(solution)/shard_map/ppermute | solution.py:10
  370.4 24.7 %collective-permute-start.5 = (bf16[512,1024]{1,0:T(8,128)(2,1)S(1)}, bf16[512,1024]{1,0:T(8,128)(2,1)S(1)}, u32[]{:S(2)}, u32[]{:S(2)}) collective-permute-start(bf16[512,1024]{1,0:T(8,128)(2,1)S(1)} %bitcast.162), channel_id=1, source_target_pairs={{0,8},{8,16},{16,24},{1,9},{9,17},{17,25},{2,10},{10,18},{18,26},{... | collective-permute-start | bytes 3145736 | tf_op jit(solution)/shard_map/ppermute | solution.py:10
  403.7 31.4 %all-to-all-start = ((f32[4,1,512]{2,1,0:T(1,128)}), f32[4,1,512]{2,1,0:T(1,128)S(1)}, u32[]{:S(2)}, u32[]{:S(2)}) async-start(f32[4,1,512]{2,1,0:T(1,128)} %constant_dynamic-update-slice_fusion), calls=%async_computation | async-start | bytes 16384 | tf_op jit(solution)/shard_map/all_to_all | solution.py:73
  435.1 0.6 copy-start.5
Sparse Core Ops, SparseCore 0:
  9.6 149.4 all-gather.2
